TPU v7x, 256 devices: a whole 4x4x8 slice. The times are simulated.
256 devices in a mesh: row: 16 (over z_lo, x, core), col: 16 (over y, z_hi).
Axes of the slice: x: 4, y: 4, z: 8 (z_hi: 4, z_lo: 2; z = z_hi * 2 + z_lo), core: 2. Of those that a mesh axis runs over, the one named last changes fastest.
Arguments:
- object_slices: float32 [4, 2, 4096, 4096], P(None, None, 'row', 'col'), may hold values from -2.5 to 2.5
- probe_wave: float32 [2, 128, 128], replicated, may hold values from -4 to 4
- offsets: int32 [16, 16, 4, 2], P('row', 'col'), may hold values from 0 to 255
- active_flags: int32 [16, 16, 4], P('row', 'col'), may hold values 0 or 1
- intensity: float32 [16, 16, 4, 128, 128], P('row', 'col'), may hold values from 0.1 to 3
Outputs:
- updated_object: float32 [4, 2, 4096, 4096], P(None, None, 'row', 'col')
- updated_probe: float32 [2, 128, 128], replicated
Inputs may be any that keep to these rules, and one draw needn't show every extreme that they name: `offsets`: each position's centre lies in its own device's tile; its window may reach into neighbouring tiles, diagonal ones included. `active_flags`: positions with flag 0 contribute nothing.
All inputs are finite; a program needn't handle non-finite values. No bound on the sum of `active_flags` on one device may be relied on, other than what follows from the above.
Results may differ from a plain program's by a relative error of at most 0.00018.
Values sent between devices are 32-bit elements; how exact they have to be, the bound alone decides.
A program may use at most 64 MiB of HBM per device.

v0:
```python
import math
import jax
import jax.numpy as jnp
from jax import lax
from jax.sharding import PartitionSpec as P

fresnel_phase = 40.0
object_step = 0.25
exact = lax.Precision.HIGHEST


def padded_2(cells, sides, width):
    for axis, dim in sides:
        count = lax.axis_size(axis)
        head = lax.slice_in_dim(cells, 0, width, axis=dim)
        tail = lax.slice_in_dim(cells, cells.shape[dim] - width, cells.shape[dim], axis=dim)
        cells = jnp.concatenate(
            [
                lax.ppermute(tail, axis, [(i, (i + 1) % count) for i in range(count)]),
                cells,
                lax.ppermute(head, axis, [((i + 1) % count, i) for i in range(count)]),
            ],
            axis=dim,
        )
    return cells


def passed_along(array, axis, by):
    length = lax.axis_size(axis)
    return lax.ppermute(array, axis, [(i, (i + by) % length) for i in range(length)])


def dft_tables(extent):
    indices = jnp.arange(extent, dtype=jnp.int32)
    angles = (indices[:, None] * indices[None, :] % extent).astype(jnp.float32) * (
        2.0 * jnp.pi / extent
    )
    norming = 1.0 / math.sqrt(extent)
    cosine = jnp.cos(angles) * norming
    sine_part = -jnp.sin(angles) * norming
    forward = jnp.stack([jnp.stack([cosine, -sine_part]), jnp.stack([sine_part, cosine])])
    backward = jnp.stack([jnp.stack([cosine, sine_part]), jnp.stack([-sine_part, cosine])])
    return (forward, backward)


def transfer(extent):
    indices = jnp.arange(extent, dtype=jnp.int32)
    frequency = ((indices + extent // 2) % extent - extent // 2).astype(jnp.float32) / extent
    phase_angle = -jnp.pi * fresnel_phase * (frequency[:, None] ** 2 + frequency[None, :] ** 2)
    return (jnp.cos(phase_angle), jnp.sin(phase_angle))


def transform(field_pair, tables, inverse):
    block = tables[1] if inverse else tables[0]
    stacked = jnp.stack(field_pair)
    left = jnp.einsum("pqjk,qbkl->pbjl", block, stacked, precision=exact)
    result = jnp.einsum("qbjk,pqkl->pbjl", left, block, precision=exact)
    return (result[0], result[1])


def complex_times(first, second):
    return (
        first[0] * second[0] - first[1] * second[1],
        first[0] * second[1] + first[1] * second[0],
    )


def conj_times(first, second):
    return (
        first[0] * second[0] + first[1] * second[1],
        first[0] * second[1] - first[1] * second[0],
    )


def propagate(field_pair, tables, kernel, adjoint):
    spectrum = transform(field_pair, tables, False)
    if adjoint:
        spectrum = conj_times(kernel, spectrum)
    else:
        spectrum = complex_times(kernel, spectrum)
    return transform(spectrum, tables, True)


def fetch_rim(object_slices, margin):
    return padded_2(object_slices, (("row", 2), ("col", 3)), margin)


def body(object_slices, probe_wave, offsets, active_flags, intensity):
    extent = probe_wave.shape[-1]
    margin = extent // 2
    layers = object_slices.shape[0]
    positions = offsets.shape[2]
    padded = fetch_rim(object_slices, margin)
    start_rows = offsets[0, 0, :, 0]
    start_cols = offsets[0, 0, :, 1]
    anchor = jnp.zeros((), jnp.int32)

    def window_at(source, top_row, left_col):
        return lax.dynamic_slice(
            source, (anchor, anchor, top_row, left_col), (layers, 2, extent, extent)
        )

    windows = jax.vmap(window_at, in_axes=(None, 0, 0))(padded, start_rows, start_cols)
    tables = dft_tables(extent)
    kernel = transfer(extent)
    flags = active_flags[0, 0].astype(jnp.float32)[:, None, None]
    observed = intensity[0, 0]
    wavefield = (
        jnp.broadcast_to(probe_wave[0], (positions, extent, extent)),
        jnp.broadcast_to(probe_wave[1], (positions, extent, extent)),
    )
    incident = []
    for layer_at in range(layers):
        incident.append(wavefield)
        transmit = (windows[:, layer_at, 0], windows[:, layer_at, 1])
        wavefield = complex_times(wavefield, transmit)
        if layer_at + 1 < layers:
            wavefield = propagate(wavefield, tables, kernel, False)
    far_field = transform(wavefield, tables, False)
    excess = flags * (far_field[0] ** 2 + far_field[1] ** 2 - observed)
    back_field = transform((excess * far_field[0], excess * far_field[1]), tables, True)
    grad_layers = [None] * layers
    for layer_at in reversed(range(layers)):
        transmit = (windows[:, layer_at, 0], windows[:, layer_at, 1])
        grad_layers[layer_at] = conj_times(incident[layer_at], back_field)
        back_field = conj_times(transmit, back_field)
        if layer_at > 0:
            back_field = propagate(back_field, tables, kernel, True)
    stacked = jnp.stack([jnp.stack(grad_pair, axis=1) for grad_pair in grad_layers], axis=1)

    def deposit(index_k, running):
        begin = (anchor, anchor, start_rows[index_k], start_cols[index_k])
        piece = stacked[index_k]
        return lax.dynamic_update_slice(
            running, lax.dynamic_slice(running, begin, piece.shape) + piece, begin
        )

    grad_pad = lax.fori_loop(0, positions, deposit, jnp.zeros_like(padded))
    from_right = passed_along(grad_pad[:, :, :, :margin], "col", -1)
    from_left = passed_along(grad_pad[:, :, :, -margin:], "col", 1)
    inner = grad_pad[:, :, :, margin:-margin]
    inner = inner.at[:, :, :, -margin:].add(from_right)
    inner = inner.at[:, :, :, :margin].add(from_left)
    from_below = passed_along(inner[:, :, :margin], "row", -1)
    from_above = passed_along(inner[:, :, -margin:], "row", 1)
    folded = inner[:, :, margin:-margin]
    folded = folded.at[:, :, -margin:].add(from_below)
    folded = folded.at[:, :, :margin].add(from_above)
    updated_object = object_slices - object_step * folded
    local_grad = jnp.stack([jnp.sum(back_field[0], axis=0), jnp.sum(back_field[1], axis=0)])
    devices = lax.axis_size("row") * lax.axis_size("col")
    factor = 1.0 / math.sqrt(positions * devices)
    summed = lax.psum(local_grad, ("row", "col"))
    updated_probe = probe_wave - factor * summed
    return (updated_object, updated_probe)


def solution(mesh):
    in_specs = (
        P(None, None, "row", "col"),
        P(),
        P("row", "col", None, None),
        P("row", "col", None),
        P("row", "col", None, None, None),
    )
    out_specs = (P(None, None, "row", "col"), P())
    return jax.shard_map(body, mesh=mesh, in_specs=in_specs, out_specs=out_specs, check_vma=False)
```

profile of v0, /device:TPU:2, one launch (start us, length us, event | category | flops | bytes accessed | tf_op | source)
XLA Modules:
  0.0 511.6 jit_solution(18418235282657406992)
XLA Ops:
  14.5 4.0 collective-permute-done
  18.4 2.4 copy.52
  20.8 2.3 copy.54
  25.1 3.3 collective-permute-start.2
  28.4 5.6 %collective-permute-start.3 = (f32[4,2,384,64]{2,3,1,0:T(8,128)S(1)}, f32[4,2,384,64]{2,3,1,0:T(8,128)S(1)}, u32[]{:S(2)}, u32[]{:S(2)}) collective-permute-start(f32[4,2,384,64]{2,3,1,0:T(8,128)S(1)} %get-tuple-element.205), channel_id=1, source_target_pairs={{1,0},{2,1},{3,2},{4,3},{5,4},{6,5},{7,6},{8,7},{9,8},{10,9},{11,1... | collective-permute-start | bytes 2359304 | tf_op jit(solution)/shard_map/ppermute | solution.py:21
  34.4 22.7 %collective-permute-done.2 = f32[4,2,384,64]{2,3,1,0:T(8,128)S(1)} collective-permute-done((f32[4,2,384,64]{2,3,1,0:T(8,128)S(1)}, f32[4,2,384,64]{2,3,1,0:T(8,128)S(1)}, u32[]{:S(2)}, u32[]{:S(2)}) %collective-permute-start.2) | collective-permute-done | bytes 786464 | tf_op jit(solution)/shard_map/ppermute | solution.py:19
  57.1 9.4 %collective-permute-done.3 = f32[4,2,384,64]{2,3,1,0:T(8,128)S(1)} collective-permute-done((f32[4,2,384,64]{2,3,1,0:T(8,128)S(1)}, f32[4,2,384,64]{2,3,1,0:T(8,128)S(1)}, u32[]{:S(2)}, u32[]{:S(2)}) %collective-permute-start.3) | collective-permute-done | bytes 786464 | tf_op jit(solution)/shard_map/ppermute | solution.py:21
  66.5 3.2 pad_maximum_fusion
  69.7 18.9 %while.19 = (s32[]{:T(128)}, f32[4,2,384,384]{2,3,1,0:T(8,128)}, s32[4,4]{1,0:T(4,128)S(1)}, f32[4,4,2,128,128]{3,4,0,2,1:T(8,128)}, s32[]{:T(128)}) while((s32[]{:T(128)}, f32[4,2,384,384]{2,3,1,0:T(8,128)}, s32[4,4]{1,0:T(4,128)S(1)}, f32[4,4,2,128,128]{3,4,0,2,1:T(8,128)}, s32[]{:T(128)}) %tuple.107), condition=%wide.while_cond.4, body=%wide.while_body.4.sunk | while | flops 2 | bytes 4194437 | solution.py:99
  70.4 2.8 constant_dynamic-slice_fusion.11
  75.1 2.8 constant_dynamic-slice_fusion.11
  79.8 2.8 constant_dynamic-slice_fusion.11
  84.5 2.8 constant_dynamic-slice_fusion.11
  111.4 2.5 broadcast_in_dim.10.clone
  113.9 64.0 %while.18 = (s32[]{:T(128)}, f32[4,2,384,384]{2,3,1,0:T(8,128)}, s32[4]{0:T(128)S(1)}, s32[4]{0:T(128)S(1)}, f32[4,4,2,128,128]{3,4,0,2,1:T(8,128)}, /*index=5*/s32[]{:T(128)}, s32[]{:T(128)}, s32[]{:T(128)}) while((s32[]{:T(128)}, f32[4,2,384,384]{2,3,1,0:T(8,128)}, s32[4]{0:T(128)S(1)}, s32[4]{0:T(128)S(1)}, ...), condition=%wide.region_1.2_spmd, body=%wide.region_0.1_spmd.sunk | while | flops 131080 | bytes 7864521 | solution.py:138
  122.2 7.7 %dynamic_update_slice.8 = f32[4,2,384,384]{2,3,1,0:T(8,128)} dynamic-update-slice(f32[4,2,384,384]{2,3,1,0:T(8,128)} %get-tuple-element.352, f32[4,2,128,128]{2,3,1,0:T(8,128)S(1)} %copy.304, s32[]{:T(128)} %constant.169.clone.1..sunk, s32[]{:T(128)} %constant.169.clone.1..sunk, s32[]{:T(128)S(6)} %select_n.167, s32[]{:T(128)S(6)} %select_n.168) | dynamic-update-slice | bytes 1048580 | tf_op jit(solution)/shard_map/while/body/eval_jaxpr/dynamic_update_slice | solution.py:134
  138.2 7.7 %dynamic_update_slice.8 = f32[4,2,384,384]{2,3,1,0:T(8,128)} dynamic-update-slice(f32[4,2,384,384]{2,3,1,0:T(8,128)} %get-tuple-element.352, f32[4,2,128,128]{2,3,1,0:T(8,128)S(1)} %copy.304, s32[]{:T(128)} %constant.169.clone.1..sunk, s32[]{:T(128)} %constant.169.clone.1..sunk, s32[]{:T(128)S(6)} %select_n.167, s32[]{:T(128)S(6)} %select_n.168) | dynamic-update-slice | bytes 1048580 | tf_op jit(solution)/shard_map/while/body/eval_jaxpr/dynamic_update_slice | solution.py:134
  154.2 7.7 %dynamic_update_slice.8 = f32[4,2,384,384]{2,3,1,0:T(8,128)} dynamic-update-slice(f32[4,2,384,384]{2,3,1,0:T(8,128)} %get-tuple-element.352, f32[4,2,128,128]{2,3,1,0:T(8,128)S(1)} %copy.304, s32[]{:T(128)} %constant.169.clone.1..sunk, s32[]{:T(128)} %constant.169.clone.1..sunk, s32[]{:T(128)S(6)} %select_n.167, s32[]{:T(128)S(6)} %select_n.168) | dynamic-update-slice | bytes 1048580 | tf_op jit(solution)/shard_map/while/body/eval_jaxpr/dynamic_update_slice | solution.py:134
  170.2 7.7 %dynamic_update_slice.8 = f32[4,2,384,384]{2,3,1,0:T(8,128)} dynamic-update-slice(f32[4,2,384,384]{2,3,1,0:T(8,128)} %get-tuple-element.352, f32[4,2,128,128]{2,3,1,0:T(8,128)S(1)} %copy.304, s32[]{:T(128)} %constant.169.clone.1..sunk, s32[]{:T(128)} %constant.169.clone.1..sunk, s32[]{:T(128)S(6)} %select_n.167, s32[]{:T(128)S(6)} %select_n.168) | dynamic-update-slice | bytes 1048580 | tf_op jit(solution)/shard_map/while/body/eval_jaxpr/dynamic_update_slice | solution.py:134
  179.4 5.3 %collective-permute-start.4 = (f32[4,2,384,64]{2,3,1,0:T(8,128)S(1)}, f32[4,2,384,64]{2,3,1,0:T(8,128)S(1)}, u32[]{:S(2)}, u32[]{:S(2)}) collective-permute-start(f32[4,2,384,64]{2,3,1,0:T(8,128)S(1)} %get-tuple-element.203), channel_id=1, source_target_pairs={{0,15},{1,0},{2,1},{3,2},{4,3},{5,4},{6,5},{7,6},{8,7},{9,8},{10,9... | collective-permute-start | bytes 2359304 | tf_op jit(solution)/shard_map/ppermute | solution.py:30
  186.8 28.9 %collective-permute-done.4 = f32[4,2,384,64]{2,3,1,0:T(8,128)S(1)} collective-permute-done((f32[4,2,384,64]{2,3,1,0:T(8,128)S(1)}, f32[4,2,384,64]{2,3,1,0:T(8,128)S(1)}, u32[]{:S(2)}, u32[]{:S(2)}) %collective-permute-start.4) | collective-permute-done | bytes 786464 | tf_op jit(solution)/shard_map/ppermute | solution.py:30
  217.0 4.1 collective-permute-done.5
  223.0 2.3 copy.116
  227.4 2.3 copy.118
  230.3 243.6 %all-reduce.2.cloned.1.call-done = f32[2,128,128]{1,2,0:T(8,128)} async-done(((f32[2,128,128]{1,2,0:T(8,128)}), f32[2,128,128]{1,2,0:T(8,128)}) %all-reduce.2.cloned.1.call-update) | async-done | bytes 131088 | tf_op jit(solution)/shard_map/psum | solution.py:153
  477.5 2.4 copy.117
  479.9 2.3 slice_add_fusion.1
  482.2 6.5 %scatter-add.16 = f32[4,2,256,256]{2,3,1,0:T(8,128)} dynamic-update-slice(f32[4,2,256,256]{2,3,1,0:T(8,128)} %slice.378, f32[4,2,64,256]{2,3,1,0:T(8,128)} %slice_add_fusion.1, s32[]{:T(128)} %constant.169.clone.1, s32[]{:T(128)} %constant.169.clone.1, s32[]{:T(128)} %constant.180.clone.1, s32[]{:T(128)} %constant.169.clone.1) | dynamic-update-slice | bytes 1048580 | tf_op jit(solution)/shard_map/scatter-add | solution.py:147
  488.7 2.4 copy.119
  492.9 5.8 %scatter-add.19 = f32[4,2,256,256]{2,3,1,0:T(8,128)} dynamic-update-slice(f32[4,2,256,256]{2,3,1,0:T(8,128)} %scatter-add.16, f32[4,2,64,256]{2,3,1,0:T(8,128)S(1)} %slice_add_fusion, s32[]{:T(128)} %constant.169.clone.1, s32[]{:T(128)} %constant.169.clone.1, s32[]{:T(128)} %constant.169.clone.1, s32[]{:T(128)} %constant.169.clone.1) | dynamic-update-slice | bytes 1048580 | tf_op jit(solution)/shard_map/scatter-add | solution.py:148
  498.7 3.2 multiply_subtract_fusion
  501.9 2.9 copy.122
  (163 shorter events, 72.1 us)
Async XLA Ops:
  7.2 466.7 %all-reduce.2.cloned.1.call-start = ((), (), s32[]{:S(2)}) async-start(), calls=%async_computation | async-start | bytes 262144 | tf_op jit(solution)/shard_map/psum | solution.py:153
  9.5 8.9 %collective-permute-start = (f32[4,2,64,256]{3,2,1,0:T(8,128)}, f32[4,2,64,256]{3,2,1,0:T(8,128)}, u32[]{:S(2)}, u32[]{:S(2)}) collective-permute-start(f32[4,2,64,256]{3,2,1,0:T(8,128)} %get-tuple-element.222), channel_id=1, source_target_pairs={{0,16},{16,32},{32,48},{48,64},{64,80},{80,96},{96,112},{112,128},... | collective-permute-start | bytes 1572872 | tf_op jit(solution)/shard_map/ppermute | solution.py:19
  9.5 11.3 %collective-permute-start.1 = (f32[4,2,64,256]{3,2,1,0:T(8,128)}, f32[4,2,64,256]{3,2,1,0:T(8,128)}, u32[]{:S(2)}, u32[]{:S(2)}) collective-permute-start(f32[4,2,64,256]{3,2,1,0:T(8,128)} %get-tuple-element.223), channel_id=1, source_target_pairs={{16,0},{32,16},{48,32},{64,48},{80,64},{96,80},{112,96},{128,112},... | collective-permute-start | bytes 1572872 | tf_op jit(solution)/shard_map/ppermute | solution.py:21
  11.2 2.0 copy-start.8
  11.2 2.2 copy-start.6
  11.2 2.5 copy-start.7
  11.2 3.2 copy-start.9
  13.2 53.3 %copy-start = (f32[4,2,256,256]{2,3,1,0:T(8,128)}, f32[4,2,256,256]{2,3,1,0:T(8,128)S(1)}, u32[]{:S(2)}) copy-start(f32[4,2,256,256]{2,3,1,0:T(8,128)S(1)} %copy.120) | copy-start | bytes 6291460
  23.1 43.4 %copy-start.2 = (f32[4,2,64,256]{2,3,1,0:T(8,128)S(1)}, f32[4,2,64,256]{2,3,1,0:T(8,128)}, u32[]{:S(2)}) copy-start(f32[4,2,64,256]{2,3,1,0:T(8,128)} %copy.52) | copy-start | bytes 1572868
  23.1 43.4 %copy-start.3 = (f32[4,2,64,256]{2,3,1,0:T(8,128)S(1)}, f32[4,2,64,256]{2,3,1,0:T(8,128)}, u32[]{:S(2)}) copy-start(f32[4,2,64,256]{2,3,1,0:T(8,128)} %copy.54) | copy-start | bytes 1572868
  25.1 32.0 %collective-permute-start.2 = (f32[4,2,384,64]{2,3,1,0:T(8,128)S(1)}, f32[4,2,384,64]{2,3,1,0:T(8,128)S(1)}, u32[]{:S(2)}, u32[]{:S(2)}) collective-permute-start(f32[4,2,384,64]{2,3,1,0:T(8,128)S(1)} %get-tuple-element.204), channel_id=1, source_target_pairs={{0,1},{1,2},{2,3},{3,4},{4,5},{5,6},{6,7},{7,8},{8,9},{9,10},{10,1... | collective-permute-start | bytes 2359304 | tf_op jit(solution)/shard_map/ppermute | solution.py:19
  28.4 38.1 %collective-permute-start.3 = (f32[4,2,384,64]{2,3,1,0:T(8,128)S(1)}, f32[4,2,384,64]{2,3,1,0:T(8,128)S(1)}, u32[]{:S(2)}, u32[]{:S(2)}) collective-permute-start(f32[4,2,384,64]{2,3,1,0:T(8,128)S(1)} %get-tuple-element.205), channel_id=1, source_target_pairs={{1,0},{2,1},{3,2},{4,3},{5,4},{6,5},{7,6},{8,7},{9,8},{10,9},{11,1... | collective-permute-start | bytes 2359304 | tf_op jit(solution)/shard_map/ppermute | solution.py:21
  91.0 1.6 copy-start.4
  109.1 0.8 copy-start.5
  179.4 36.3 %collective-permute-start.4 = (f32[4,2,384,64]{2,3,1,0:T(8,128)S(1)}, f32[4,2,384,64]{2,3,1,0:T(8,128)S(1)}, u32[]{:S(2)}, u32[]{:S(2)}) collective-permute-start(f32[4,2,384,64]{2,3,1,0:T(8,128)S(1)} %get-tuple-element.203), channel_id=1, source_target_pairs={{0,15},{1,0},{2,1},{3,2},{4,3},{5,4},{6,5},{7,6},{8,7},{9,8},{10,9... | collective-permute-start | bytes 2359304 | tf_op jit(solution)/shard_map/ppermute | solution.py:30
  184.7 36.4 %collective-permute-start.5 = (f32[4,2,384,64]{2,3,1,0:T(8,128)S(1)}, f32[4,2,384,64]{2,3,1,0:T(8,128)S(1)}, u32[]{:S(2)}, u32[]{:S(2)}) collective-permute-start(f32[4,2,384,64]{2,3,1,0:T(8,128)S(1)} %get-tuple-element.202), channel_id=1, source_target_pairs={{0,1},{1,2},{2,3},{3,4},{4,5},{5,6},{6,7},{7,8},{8,9},{9,10},{10,1... | collective-permute-start | bytes 2359304 | tf_op jit(solution)/shard_map/ppermute | solution.py:30
  225.3 252.1 %collective-permute-start.6 = (f32[4,2,64,256]{3,2,1,0:T(8,128)}, f32[4,2,64,256]{3,2,1,0:T(8,128)}, u32[]{:S(2)}, u32[]{:S(2)}) collective-permute-start(f32[4,2,64,256]{3,2,1,0:T(8,128)} %copy.116), channel_id=1, source_target_pairs={{0,240},{16,0},{32,16},{48,32},{64,48},{80,64},{96,80},{112,96},{1... | collective-permute-start | bytes 1572872 | tf_op jit(solution)/shard_map/ppermute | solution.py:30
  229.8 258.9 %collective-permute-start.7 = (f32[4,2,64,256]{3,2,1,0:T(8,128)}, f32[4,2,64,256]{3,2,1,0:T(8,128)}, u32[]{:S(2)}, u32[]{:S(2)}) collective-permute-start(f32[4,2,64,256]{3,2,1,0:T(8,128)} %copy.118), channel_id=1, source_target_pairs={{0,16},{16,32},{32,48},{48,64},{64,80},{80,96},{96,112},{112,128},... | collective-permute-start | bytes 1572872 | tf_op jit(solution)/shard_map/ppermute | solution.py:30
  491.0 7.6 %copy-start.1 = (f32[4,2,256,256]{2,3,1,0:T(8,128)S(1)}, f32[4,2,256,256]{2,3,1,0:T(8,128)}, u32[]{:S(2)}) copy-start(f32[4,2,256,256]{2,3,1,0:T(8,128)} %copy-done) | copy-start | bytes 6291460
Sparse Core Ops, SparseCore 0:
  227.4 246.3 all-reduce.1
where the time goes:
time: 515 us; the launch traced here: 512 us
  waiting for transfers between devices  313 us (61%)
  local copies, waits for them, and re-layouts  113 us (22%)
  other arithmetic  21.8 us (4%)
  matrix products  17.7 us (3%)
  starting transfers between devices  16.5 us (3%)
  loops' own time  15.5 us (3%)
  between operations  14.6 us (3%)
    psum x1, waiting for transfers between devices, body(): summed = lax.psum(local_grad, ('row', 'col'))  244 us
    ppermute x4, waiting for transfers between devices, passed_along(): lax.ppermute(array, axis, [(i, (i + by) % length) for i in range(length)])  33 us
    dynamic_update_slice x8, local copies, waits for them, and re-layouts, deposit(): lax.dynamic_update_slice(running, lax.dynamic_slice(running, begin, piece...  31.6 us
    ppermute x2, waiting for transfers between devices, padded_2(): lax.ppermute(tail, axis, [(i, (i + 1) % count) for i in range(count)])  26.7 us
    gather x24, local copies, waits for them, and re-layouts  18.8 us
    another operation x1, loops' own time, body(): grad_pad = lax.fori_loop(0, positions, deposit, jnp.zeros_like(padded))  15.4 us
  transfers between devices with their start and end apart: 9, of which 6 were waited for; matrix products, arithmetic and copies ran while one was open for 6% of the time, Pallas kernels for 0%

commit v1 on v0

--- a/solution.py
+++ b/solution.py
@@ -150,7 +150,7 @@
     local_grad = jnp.stack([jnp.sum(back_field[0], axis=0), jnp.sum(back_field[1], axis=0)])
     devices = lax.axis_size("row") * lax.axis_size("col")
     factor = 1.0 / math.sqrt(positions * devices)
-    summed = lax.psum(local_grad, ("row", "col"))
+    summed = jnp.sum(lax.all_gather(local_grad, ("row", "col")), axis=0)
     updated_probe = probe_wave - factor * summed
     return (updated_object, updated_probe)
 

time: 515 us -> 910 us (1.77); the launches traced: 512 us -> 895 us
  waiting for transfers between devices: 313 us -> 690 us
  other arithmetic: 21.8 us -> 32.7 us
    all_gather x0 -> x1, waiting for transfers between devices: none -> 605 us  [body(): summed = jnp.sum(lax.all_gather(local_grad, ('row', 'col')), axis=0)]
    psum x1 -> x0, waiting for transfers between devices: 244 us -> none  [body(): summed = lax.psum(local_grad, ('row', 'col'))]
    ppermute x2, waiting for transfers between devices: 9.39 us -> 36.7 us  [padded_2(): lax.ppermute(head, axis, [((i + 1) % count, i) for i in range(count)])]
    ppermute x2, waiting for transfers between devices: 26.7 us -> 6.08 us  [padded_2(): lax.ppermute(tail, axis, [(i, (i + 1) % count) for i in range(count)])]
    reduce_sum x0 -> x1, other arithmetic: none -> 12.3 us  [body(): summed = jnp.sum(lax.all_gather(local_grad, ('row', 'col')), axis=0)]
    ppermute x4, waiting for transfers between devices: 33 us -> 42.3 us  [passed_along(): lax.ppermute(array, axis, [(i, (i + by) % length) for i in range(length)])]
  transfers between devices with their start and end apart: 9 -> 9, of which waited for: 6 -> 7; matrix products, arithmetic and copies ran while one was open for 6% -> 11% of each run, Pallas kernels for 0% -> 0%
where the time goes in v1:
time: 910 us; the launch traced here: 895 us
  waiting for transfers between devices  690 us (76%)
  local copies, waits for them, and re-layouts  112 us (12%)
  other arithmetic  32.7 us (4%)
  matrix products  17.7 us (2%)
  loops' own time  15.3 us (2%)
  between operations  14.7 us (2%)
  starting transfers between devices  12.8 us (1%)
    all_gather x1, waiting for transfers between devices, body(): summed = jnp.sum(lax.all_gather(local_grad, ('row', 'col')), axis=0)  605 us
    ppermute x4, waiting for transfers between devices, passed_along(): lax.ppermute(array, axis, [(i, (i + by) % length) for i in range(length)])  42.3 us
    ppermute x2, waiting for transfers between devices, padded_2(): lax.ppermute(head, axis, [((i + 1) % count, i) for i in range(count)])  36.7 us
    dynamic_update_slice x8, local copies, waits for them, and re-layouts, deposit(): lax.dynamic_update_slice(running, lax.dynamic_slice(running, begin, piece...  31.8 us
    gather x24, local copies, waits for them, and re-layouts  18.5 us
  transfers between devices with their start and end apart: 9, of which 7 were waited for; matrix products, arithmetic and copies ran while one was open for 11% of the time, Pallas kernels for 0%

profile of v1, /device:TPU:2, one launch (start us, length us, event | category | flops | bytes accessed | tf_op | source)
XLA Modules:
  0.0 895.5 jit_solution(6607399223395295020)
XLA Ops:
  13.1 3.4 collective-permute-done.1
  16.5 2.4 copy.53
  19.0 2.4 copy.51
  23.4 8.7 collective-permute-start.3
  32.5 33.3 %collective-permute-done.3 = f32[4,2,384,64]{2,3,1,0:T(8,128)S(1)} collective-permute-done((f32[4,2,384,64]{2,3,1,0:T(8,128)S(1)}, f32[4,2,384,64]{2,3,1,0:T(8,128)S(1)}, u32[]{:S(2)}, u32[]{:S(2)}) %collective-permute-start.3) | collective-permute-done | bytes 786464 | tf_op jit(solution)/shard_map/ppermute | solution.py:21
  65.8 6.0 collective-permute-done.2
  71.8 3.2 pad_maximum_fusion
  75.0 18.6 %while.19 = (s32[]{:T(128)}, f32[4,2,384,384]{2,3,1,0:T(8,128)}, s32[4,4]{1,0:T(4,128)S(1)}, f32[4,4,2,128,128]{3,4,0,2,1:T(8,128)}, s32[]{:T(128)}) while((s32[]{:T(128)}, f32[4,2,384,384]{2,3,1,0:T(8,128)}, s32[4,4]{1,0:T(4,128)S(1)}, f32[4,4,2,128,128]{3,4,0,2,1:T(8,128)}, s32[]{:T(128)}) %tuple.107), condition=%wide.while_cond.4, body=%wide.while_body.4.sunk | while | flops 2 | bytes 4194437 | solution.py:99
  75.6 2.7 constant_dynamic-slice_fusion.11
  80.3 2.7 constant_dynamic-slice_fusion.11
  84.9 2.7 constant_dynamic-slice_fusion.11
  89.5 2.7 constant_dynamic-slice_fusion.11
  117.3 2.6 broadcast_in_dim.10.clone
  119.9 64.3 %while.18 = (s32[]{:T(128)}, f32[4,2,384,384]{2,3,1,0:T(8,128)}, s32[4]{0:T(128)S(1)}, s32[4]{0:T(128)S(1)}, f32[4,4,2,128,128]{3,4,0,2,1:T(8,128)}, /*index=5*/s32[]{:T(128)}, s32[]{:T(128)}, s32[]{:T(128)}) while((s32[]{:T(128)}, f32[4,2,384,384]{2,3,1,0:T(8,128)}, s32[4]{0:T(128)S(1)}, s32[4]{0:T(128)S(1)}, ...), condition=%wide.region_1.2_spmd, body=%wide.region_0.1_spmd.sunk | while | flops 131080 | bytes 7864521 | solution.py:138
  128.3 7.8 dynamic_update_slice.8
  144.3 7.7 dynamic_update_slice.8
  160.4 7.8 dynamic_update_slice.8
  176.5 7.8 dynamic_update_slice.8
  186.1 2.6 collective-permute-start.5
  190.9 38.0 %collective-permute-done.4 = f32[4,2,384,64]{2,3,1,0:T(8,128)S(1)} collective-permute-done((f32[4,2,384,64]{2,3,1,0:T(8,128)S(1)}, f32[4,2,384,64]{2,3,1,0:T(8,128)S(1)}, u32[]{:S(2)}, u32[]{:S(2)}) %collective-permute-start.4) | collective-permute-done | bytes 786464 | tf_op jit(solution)/shard_map/ppermute | solution.py:30
  232.0 2.3 copy.115
  234.3 2.3 copy.117
  239.1 4.3 collective-permute-done.6
  243.4 2.4 copy.116
  245.8 2.3 slice_add_fusion.1
  248.1 6.5 scatter-add.16
  254.6 2.4 copy.118
  258.8 5.8 scatter-add.19
  264.6 3.2 multiply_subtract_fusion
  267.8 2.9 copy.121
  270.7 605.0 %all-gather.3.cloned.1.call-done = f32[512,128,128]{2,1,0:T(8,128)} async-done(((f32[2,128,128]{2,1,0:T(8,128)}), f32[512,128,128]{2,1,0:T(8,128)}) %all-gather.3.cloned.1.call-update) | async-done | bytes 33554448 | tf_op jit(solution)/shard_map/all_gather | solution.py:153
  875.7 12.3 %reduce_sum.29 = f32[2,128,128]{2,1,0:T(8,128)S(1)} reduce(f32[256,2,128,128]{3,2,1,0:T(8,128)} %bitcast.518, f32[]{:T(128)} %constant.170.clone.1), dimensions={0}, to_apply=%region_4.5 | reduce | flops 8355840 | bytes 33685508 | tf_op jit(solution)/shard_map/reduce_sum | solution.py:153
  (173 shorter events, 69.4 us)
Async XLA Ops:
  7.2 868.5 %all-gather.3.cloned.1.call-start = ((), (), s32[]{:S(2)}) async-start(), calls=%async_computation | async-start | bytes 33685504 | tf_op jit(solution)/shard_map/all_gather | solution.py:153
  9.5 7.0 collective-permute-start.1
  9.5 2.5 copy-start.12
  9.5 2.6 copy-start.13
  9.5 2.8 copy-start.10
  9.5 9.5 %collective-permute-start = (f32[4,2,64,256]{3,2,1,0:T(8,128)}, f32[4,2,64,256]{3,2,1,0:T(8,128)}, u32[]{:S(2)}, u32[]{:S(2)}) collective-permute-start(f32[4,2,64,256]{3,2,1,0:T(8,128)} %get-tuple-element.222), channel_id=1, source_target_pairs={{0,16},{16,32},{32,48},{48,64},{64,80},{80,96},{96,112},{112,128},... | collective-permute-start | bytes 1572872 | tf_op jit(solution)/shard_map/ppermute | solution.py:19
  11.9 59.8 %copy-start = (f32[4,2,256,256]{2,3,1,0:T(8,128)}, f32[4,2,256,256]{2,3,1,0:T(8,128)S(1)}, u32[]{:S(2)}) copy-start(f32[4,2,256,256]{2,3,1,0:T(8,128)S(1)} %copy.119) | copy-start | bytes 6291460
  12.4 81.1 %copy-start.6 = (f32[128,128]{0,1:T(8,128)}, f32[128,128]{0,1:T(8,128)S(1)}, u32[]{:S(2)}) copy-start(f32[128,128]{0,1:T(8,128)S(1)} %copy.62) | copy-start | bytes 196612
  12.5 81.0 %copy-start.8 = (f32[128,128]{0,1:T(8,128)}, f32[128,128]{0,1:T(8,128)S(1)}, u32[]{:S(2)}) copy-start(f32[128,128]{0,1:T(8,128)S(1)} %copy.50) | copy-start | bytes 196612
  21.4 10.7 %copy-start.14 = (s32[1,1,4]{2,1,0:T(1,128)S(1)}, s32[1,1,4]{2,1,0:T(1,128)}, u32[]{:S(2)}) copy-start(s32[1,1,4]{2,1,0:T(1,128)} %param.18) | copy-start | bytes 52
  21.4 50.4 %copy-start.2 = (f32[4,2,64,256]{2,3,1,0:T(8,128)S(1)}, f32[4,2,64,256]{2,3,1,0:T(8,128)}, u32[]{:S(2)}) copy-start(f32[4,2,64,256]{2,3,1,0:T(8,128)} %copy.53) | copy-start | bytes 1572868
  21.4 50.4 %copy-start.3 = (f32[4,2,64,256]{2,3,1,0:T(8,128)S(1)}, f32[4,2,64,256]{2,3,1,0:T(8,128)}, u32[]{:S(2)}) copy-start(f32[4,2,64,256]{2,3,1,0:T(8,128)} %copy.51) | copy-start | bytes 1572868
  23.4 42.4 %collective-permute-start.3 = (f32[4,2,384,64]{2,3,1,0:T(8,128)S(1)}, f32[4,2,384,64]{2,3,1,0:T(8,128)S(1)}, u32[]{:S(2)}, u32[]{:S(2)}) collective-permute-start(f32[4,2,384,64]{2,3,1,0:T(8,128)S(1)} %get-tuple-element.205), channel_id=1, source_target_pairs={{1,0},{2,1},{3,2},{4,3},{5,4},{6,5},{7,6},{8,7},{9,8},{10,9},{11,1... | collective-permute-start | bytes 2359304 | tf_op jit(solution)/shard_map/ppermute | solution.py:21
  32.1 39.7 %collective-permute-start.2 = (f32[4,2,384,64]{2,3,1,0:T(8,128)S(1)}, f32[4,2,384,64]{2,3,1,0:T(8,128)S(1)}, u32[]{:S(2)}, u32[]{:S(2)}) collective-permute-start(f32[4,2,384,64]{2,3,1,0:T(8,128)S(1)} %get-tuple-element.204), channel_id=1, source_target_pairs={{0,1},{1,2},{2,3},{3,4},{4,5},{5,6},{6,7},{7,8},{8,9},{9,10},{10,1... | collective-permute-start | bytes 2359304 | tf_op jit(solution)/shard_map/ppermute | solution.py:19
  95.9 1.6 copy-start.4
  114.7 1.0 copy-start.5
  114.8 1.0 copy-start.7
  114.8 1.0 copy-start.9
  185.7 43.1 %collective-permute-start.4 = (f32[4,2,384,64]{2,3,1,0:T(8,128)S(1)}, f32[4,2,384,64]{2,3,1,0:T(8,128)S(1)}, u32[]{:S(2)}, u32[]{:S(2)}) collective-permute-start(f32[4,2,384,64]{2,3,1,0:T(8,128)S(1)} %get-tuple-element.203), channel_id=1, source_target_pairs={{0,15},{1,0},{2,1},{3,2},{4,3},{5,4},{6,5},{7,6},{8,7},{9,8},{10,9... | collective-permute-start | bytes 2359304 | tf_op jit(solution)/shard_map/ppermute | solution.py:30
  186.1 44.0 %collective-permute-start.5 = (f32[4,2,384,64]{2,3,1,0:T(8,128)S(1)}, f32[4,2,384,64]{2,3,1,0:T(8,128)S(1)}, u32[]{:S(2)}, u32[]{:S(2)}) collective-permute-start(f32[4,2,384,64]{2,3,1,0:T(8,128)S(1)} %get-tuple-element.202), channel_id=1, source_target_pairs={{0,1},{1,2},{2,3},{3,4},{4,5},{5,6},{6,7},{7,8},{8,9},{9,10},{10,1... | collective-permute-start | bytes 2359304 | tf_op jit(solution)/shard_map/ppermute | solution.py:30
  234.3 9.1 %collective-permute-start.6 = (f32[4,2,64,256]{3,2,1,0:T(8,128)}, f32[4,2,64,256]{3,2,1,0:T(8,128)}, u32[]{:S(2)}, u32[]{:S(2)}) collective-permute-start(f32[4,2,64,256]{3,2,1,0:T(8,128)} %copy.115), channel_id=1, source_target_pairs={{0,240},{16,0},{32,16},{48,32},{64,48},{80,64},{96,80},{112,96},{1... | collective-permute-start | bytes 1572872 | tf_op jit(solution)/shard_map/ppermute | solution.py:30
  236.7 17.9 %collective-permute-start.7 = (f32[4,2,64,256]{3,2,1,0:T(8,128)}, f32[4,2,64,256]{3,2,1,0:T(8,128)}, u32[]{:S(2)}, u32[]{:S(2)}) collective-permute-start(f32[4,2,64,256]{3,2,1,0:T(8,128)} %copy.117), channel_id=1, source_target_pairs={{0,16},{16,32},{32,48},{48,64},{64,80},{80,96},{96,112},{112,128},... | collective-permute-start | bytes 1572872 | tf_op jit(solution)/shard_map/ppermute | solution.py:30
  257.0 7.6 copy-start.1
  875.7 12.3 %copy-start.11 = (f32[2,128,128]{2,1,0:T(8,128)S(1)}, f32[2,128,128]{2,1,0:T(8,128)}, u32[]{:S(2)}) copy-start(f32[2,128,128]{2,1,0:T(8,128)} %param.16) | copy-start | bytes 393220
Sparse Core Ops, SparseCore 0:
  115.7 759.9 all-gather.2
